TPU v7x, 32 devices: a whole 2x2x4 slice. The times are simulated.
32 devices in a mesh: vol: 8 (over z, y), pix: 4 (over x, core).
Axes of the slice: x: 2, y: 2, z: 4, core: 2. Of those that a mesh axis runs over, the one named last changes fastest.
Arguments:
- kernel: bfloat16 [524288, 128], P(('vol', 'pix')), may hold values from 0 to 0.25
- pressure: bfloat16 [524288], P(('vol', 'pix')), may hold values from 0.049804688 to 2
- velocity: bfloat16 [524288], P(('vol', 'pix')), may hold values from -4 to 4
- entry_slot: int32 [32, 16384], P(('vol', 'pix')), may hold values from 0 to 1023, never falling along the last dimension, each value on 1 to 32 neighbouring positions
- slot_tile: int32 [32, 1024], P(('vol', 'pix')), may hold values from 0 to 8191, as said below
- tile_owner: int32 [8192], replicated, may hold values from 0 to 3, as said below
Outputs:
- owned_tiles: float32 [16384, 256], P(('vol', 'pix'))
- shell_map: float32 [8192, 256], P('vol')
Inputs may be any that keep to these rules, and one draw needn't show every extreme that they name: `entry_slot`: for each device the slot numbers never fall along its 16384 crossings; every slot has at least one crossing and at most 32. `tile_owner`: within every block of 1024 consecutive tiles each pix index owns 256 // 2 to 512 tiles, and one owner of each block owns exactly 512. `slot_tile`: the 1024 tiles of one device are distinct; at most 64 of them belong to any one owning device (vol index t // 1024, pix index tile_owner[t]), and one owning device gets exactly 64 from every device.
All inputs are finite; a program needn't handle non-finite values.
Results may differ from a plain program's by a relative error of at most 0.0003.
Values sent between devices are 32-bit elements; how exact they have to be, the bound alone decides.
No kernel may reach another device: no remote copies, remote signals or barrier semaphores. Data moves between devices by JAX's collectives and lax.ppermute only.
A program may use at most 64 MiB of HBM per device.

v0:
```python
import functools

import jax
import jax.numpy as jnp
from jax import lax
from jax.experimental import pallas as pl
from jax.experimental.pallas import tpu as pltpu
from jax.sharding import PartitionSpec as P


LANES = 128
HEAD = 8
ROOM = pltpu.CompilerParams(vmem_limit_bytes=16 << 20)
GROUP = 256
WINDOW = 40
SUBS = 2


SMEM = pl.BlockSpec(memory_space=pltpu.SMEM)
VMEM = pl.BlockSpec(memory_space=pltpu.VMEM)
ANY = pl.BlockSpec(memory_space=pl.ANY)
HBM = pl.BlockSpec(memory_space=pltpu.HBM)


def iota(shape, axis):
    return lax.broadcasted_iota(jnp.int32, shape, axis)


def nt_dot(a, b):
    return lax.dot_general(a, b, (((1,), (1,)), ((), ())), preferred_element_type=jnp.float32)


def dot(a, b):
    return jnp.dot(a, b, preferred_element_type=jnp.float32)


def ones_where(mask):
    return jnp.where(mask, 1.0, 0.0).astype(jnp.bfloat16)


def bytes_of(x):
    return (x >> 8).astype(jnp.float32), (x & 255).astype(jnp.float32)


def running_counts(marks, rows):
    total = marks.shape[0]
    upper = ones_where(iota((LANES, LANES), 0) <= iota((LANES, LANES), 1))
    row, column = iota((total, total), 0), iota((total, total), 1)
    earlier = ones_where((column < row) & (row // rows == column // rows))
    before = dot(earlier, marks).astype(jnp.bfloat16)
    return dot(marks, upper) + dot(before, jnp.ones((LANES, LANES), jnp.bfloat16))


def plan_kernel(vols, parts, block, cap, both, me_ref, tile_ref, slot_ref, place_ref, ends_ref, head_ref):
    size = cap + HEAD
    part_tiles = block // parts
    lane = iota((HEAD, LANES), 1)
    line = iota((HEAD, LANES), 0)
    slots = slot_ref[...]
    ends = ones_where(((line == 0) & (lane == 0)) | ((line == 1) & (lane == LANES - 1)))
    high, low = bytes_of(slots)
    ends_ref[...] = (
        nt_dot(ends, high.astype(jnp.bfloat16)) * 256.0 + nt_dot(ends, low.astype(jnp.bfloat16))
    ).astype(jnp.int32)

    tiles = tile_ref[...]
    rows = tiles.shape[0]
    classes = vols * parts
    part = tiles // part_tiles
    group = part ^ (me_ref[0] * parts + me_ref[1])
    marks = jnp.concatenate([jnp.where(group == i, 1.0, 0.0) for i in range(classes)], axis=0)
    counts = running_counts(marks.astype(jnp.bfloat16), rows) * marks
    place = jnp.zeros((rows, LANES), jnp.float32)
    for i in range(classes):
        place = place + counts[i * rows : (i + 1) * rows]
    place = place.astype(jnp.int32) - 1
    fits = place < cap
    spilled = jnp.sum(jnp.where(fits, 0.0, 1.0), axis=(0, 1), keepdims=True)
    place = jnp.where(me_ref[2] == 0, place, cap - 1 - place)
    place_ref[...] = jnp.where(fits, group * size + place, classes * size)
    lists = -(-both // LANES)
    width = lists * LANES
    spot = jnp.where(fits, place + me_ref[2] * (both - cap), -1)
    high, low = bytes_of(tiles - part * part_tiles + 1)
    ids = jnp.zeros((2 * classes, width), jnp.float32)
    which = iota((classes, LANES), 0)
    for r in range(rows):
        here = group[r : r + 1] == which
        pieces = jnp.concatenate(
            [jnp.where(here, high[r : r + 1], 0.0), jnp.where(here, low[r : r + 1], 0.0)], axis=0
        )
        spots = ones_where(iota((width, LANES), 0) == spot[r : r + 1])
        ids = ids + nt_dot(pieces.astype(jnp.bfloat16), spots)
    ids = ids[:classes] * 256.0 + ids[classes:]
    for k in range(classes):
        held = jnp.max(counts[k * rows : (k + 1) * rows], axis=(0, 1), keepdims=True)
        head = jnp.where(line == lists, jnp.broadcast_to(spilled, (HEAD, LANES)), 0.0)
        head = jnp.where(line == lists + 1, jnp.broadcast_to(held, (HEAD, LANES)), head)
        for i in range(lists):
            head = jnp.where(line == i, ids[k : k + 1, i * LANES : (i + 1) * LANES], head)
        head_ref[k * HEAD : (k + 1) * HEAD, :] = head


def plan(me, tiles, slot, vols, parts, block, cap, both):
    rows = tiles.shape[0]
    return pl.pallas_call(
        functools.partial(plan_kernel, vols, parts, block, cap, both),
        in_specs=[SMEM, VMEM, VMEM],
        out_specs=[VMEM, VMEM, VMEM],
        out_shape=[
            jax.ShapeDtypeStruct((rows, LANES), jnp.int32),
            jax.ShapeDtypeStruct((HEAD, slot.shape[0]), jnp.int32),
            jax.ShapeDtypeStruct((vols * parts * HEAD, LANES), jnp.float32),
        ],
        compiler_params=ROOM,
        name="plan",
    )(me, tiles, slot)


def project_kernel(
    steps, cap, me_ref, ends_ref, place_ref, kernel_hbm, thermal_ref, kinetic_ref, slot_ref, head_ref,
    own_out, other_out,
    kernel_ref, own_ref, other_ref, own_stage, other_stage, own_s, other_s, in_sem
):
    entries, _ = kernel_ref.shape
    part = entries // steps
    groups = part // GROUP
    lines = GROUP // LANES
    slots = place_ref.shape[0]
    total = entries // LANES

    def load(step):
        piece = pl.ds(pl.multiple_of(step * part, part), part)
        return pltpu.make_async_copy(kernel_hbm.at[piece], kernel_ref.at[piece], in_sem.at[step])

    for step in range(steps):
        load(step).start()
    for ref in (own_ref, other_ref, own_stage, other_stage):
        ref[...] = jnp.zeros_like(ref)
    thermal, kinetic = thermal_ref[...].astype(jnp.float32), kinetic_ref[...].astype(jnp.float32)
    own_s[...] = jnp.where(me_ref[2] == 0, thermal, kinetic)
    other_s[...] = jnp.where(me_ref[2] == 0, kinetic, thermal)
    line = iota((WINDOW, LANES), 0)

    def first(group):
        return ends_ref[group * lines] & -8

    def reach(group):
        return ends_ref[total + group * lines + lines - 1] - first(group)

    def add(group, base):
        own, other = [], []
        for r in range(lines):
            at = pl.ds(group * lines + r, 1)
            match = line == slot_ref[at, :] - base
            own.append(jnp.where(match, own_s[at, :], 0.0))
            other.append(jnp.where(match, other_s[at, :], 0.0))
        weights = jnp.concatenate(
            [jnp.concatenate(own, axis=1), jnp.concatenate(other, axis=1)], axis=0
        ).astype(jnp.bfloat16)
        sums = dot(weights, kernel_ref[pl.ds(pl.multiple_of(group * GROUP, GROUP), GROUP), :])
        window = pl.ds(pl.multiple_of(base, 8), WINDOW)
        own_ref[window, :] += sums[:WINDOW]
        other_ref[window, :] += sums[WINDOW:]

    def turn(step, most):
        load(step).wait()
        for g in range(groups):
            group = step * groups + g
            add(group, first(group))
            most = jnp.maximum(most, reach(group))
        return most

    most = lax.fori_loop(0, steps, turn, 0)

    @pl.when(most >= WINDOW)
    def _():
        def more(group, carry):
            def again(w, inner):
                add(group, first(group) + w * WINDOW)
                return inner

            return lax.fori_loop(1, reach(group) // WINDOW + 1, again, carry)

        lax.fori_loop(0, steps * groups, more, 0)

    unroll = 16

    def move(i, carry):
        for u in range(unroll):
            s = i * unroll + u
            to = place_ref[s]
            own_stage[pl.ds(to, 1), :] = own_ref[pl.ds(s, 1), :]
            other_stage[pl.ds(to, 1), :] = other_ref[pl.ds(s, 1), :]
        return carry

    lax.fori_loop(0, slots // unroll, move, 0)
    size = cap + HEAD
    for out, stage in ((own_out, own_stage), (other_out, other_stage)):
        for k in range(head_ref.shape[0] // HEAD):
            at = k * size
            out[at : at + cap, :] = stage[at : at + cap, :]
            out[at + cap : at + size, :] = head_ref[k * HEAD : (k + 1) * HEAD, :]


def project(me, kernel, factors, slot, ends, place, head, cap):
    entries, pixels = kernel.shape
    slots = place.shape[0]
    steps = 4
    rows = head.shape[0] // HEAD * (cap + HEAD)
    partial = pltpu.VMEM((slots + WINDOW, pixels), jnp.float32)
    stage = pltpu.VMEM((rows + HEAD, pixels), jnp.float32)
    factor = pltpu.VMEM(slot.shape, jnp.float32)
    return pl.pallas_call(
        functools.partial(project_kernel, steps, cap),
        in_specs=[SMEM, SMEM, SMEM, HBM, VMEM, VMEM, VMEM, VMEM],
        out_specs=[VMEM] * 2,
        out_shape=[jax.ShapeDtypeStruct((rows, pixels), jnp.float32)] * 2,
        scratch_shapes=[
            pltpu.VMEM((entries, pixels), kernel.dtype),
            partial, partial, stage, stage, factor, factor,
            pltpu.SemaphoreType.DMA((steps,)),
        ],
        compiler_params=ROOM,
        name="project",
    )(me, ends, place, kernel, *factors, slot, head)


def pack_kernel(cap, both, me_ref, mine_ref, other_ref, *outs):
    size = cap + HEAD
    lists = -(-both // LANES)
    lower = me_ref[2] == 0
    line = iota((HEAD, LANES), 0)
    heads, spilled = [], jnp.zeros((1, LANES), jnp.float32)
    for k, out in enumerate(outs):
        mine, other = mine_ref[k * size : (k + 1) * size, :], other_ref[k * size : (k + 1) * size, :]
        one, two = jnp.where(lower, mine, other), jnp.where(lower, other, mine)
        out[:cap, :] = one[:cap]
        if both > 2 * cap:
            out[cap : both - cap, :] = jnp.zeros((both - 2 * cap, LANES), jnp.float32)
        shared = max(2 * cap - both, 0)
        if shared:
            out[cap - shared : cap, :] = one[cap - shared : cap] + two[:shared]
        out[cap + max(both - 2 * cap, 0) : both, :] = two[shared:cap]
        head = one[cap:] + two[cap:]
        heads.append(head)
        spilled = spilled + head[lists : lists + 1] + jnp.maximum(head[lists + 1 : lists + 2] - both, 0.0)
    for out, head in zip(outs, heads):
        out[both:, :] = jnp.where(line == lists, spilled, head)


def pack(me, mine, other, cap, both):
    count = mine.shape[0] // (cap + HEAD)
    out = jax.ShapeDtypeStruct((both + HEAD, mine.shape[1]), jnp.float32)
    return pl.pallas_call(
        functools.partial(pack_kernel, cap, both),
        in_specs=[SMEM, VMEM, VMEM],
        out_specs=[VMEM] * count,
        out_shape=[out] * count,
        compiler_params=ROOM,
        name="pack",
    )(me, mine, other)


def split(x):
    high = x.astype(jnp.bfloat16)
    return high, (x - high.astype(jnp.float32)).astype(jnp.bfloat16)


def collect_kernel(count, sub_tiles, *refs):
    messages, outs, rows_s = refs[:count], refs[count : count + SUBS], refs[count + SUBS :]
    both, pixels = messages[0].shape[0] - HEAD, messages[0].shape[1]
    lists = -(-both // LANES)
    flag = jnp.zeros((HEAD, pixels), jnp.float32)
    ids = []
    for message, rows in zip(messages, rows_s):
        rows[...] = jnp.concatenate(split(message[:both, :]), axis=1)
        head = message[both:, :]
        flag = flag + head[lists : lists + 1]
        names = jnp.concatenate([head[i : i + 1] for i in range(lists)], axis=1)[:, :both]
        ids.append(names.astype(jnp.int32) - 1)
    chunk = min(256, sub_tiles)
    for sub, out_ref in enumerate(outs):
        for t in range(0, sub_tiles, chunk):
            sums = jnp.zeros((chunk, 2 * pixels), jnp.float32)
            for names, rows in zip(ids, rows_s):
                hit = ones_where(iota((chunk, both), 0) + (sub * sub_tiles + t) == names)
                sums = sums + dot(hit, rows[...])
            out_ref[t : t + chunk, :] = sums[:, :pixels] + sums[:, pixels:]
        out_ref[sub_tiles:, :] = flag


def collect(messages, sub_tiles):
    rows, pixels = messages[0].shape
    return pl.pallas_call(
        functools.partial(collect_kernel, len(messages), sub_tiles),
        in_specs=[VMEM] * len(messages),
        out_specs=[VMEM] * SUBS,
        out_shape=[jax.ShapeDtypeStruct((sub_tiles + HEAD, pixels), jnp.float32)] * SUBS,
        scratch_shapes=[pltpu.VMEM((rows - HEAD, 2 * pixels), jnp.bfloat16)] * len(messages),
        compiler_params=ROOM,
        name="collect",
    )(*messages)


def owner_kernel(parts, me_ref, owner_ref, row_ref):
    most = row_ref.shape[1]
    owners = owner_ref[...]
    rows = owners.shape[0]
    mine = owners == me_ref[1] * 2 + me_ref[2]
    marks = jnp.where(mine, 1.0, 0.0)
    rank = running_counts(marks.astype(jnp.bfloat16), rows).astype(jnp.int32) - 1
    index = iota((rows, LANES), 0) * LANES + iota((rows, LANES), 1)
    found = jnp.zeros((HEAD, most), jnp.float32)
    line = iota((HEAD, LANES), 0)
    high, low = bytes_of(index + 1)
    for r in range(rows):
        pieces = jnp.where(line == 0, high[r : r + 1], jnp.where(line == 1, low[r : r + 1], 0.0))
        pieces = jnp.where(mine[r : r + 1], pieces, 0.0)
        spots = ones_where(iota((most, LANES), 0) == rank[r : r + 1])
        found = found + nt_dot(pieces.astype(jnp.bfloat16), spots)
    tile = (found[0:1] * 256.0 + found[1:2]).astype(jnp.int32) - 1
    tile = jnp.where(tile < 0, rows * LANES, tile)
    bounds = jnp.zeros((1, most), jnp.float32)
    for p in range(1, SUBS * parts + 1):
        before = jnp.where(index < p * (rows * LANES // (SUBS * parts)), marks, 0.0)
        bounds = jnp.where(iota((1, most), 1) == p, jnp.sum(before, axis=(0, 1), keepdims=True), bounds)
    row_ref[...] = jnp.where(iota((HEAD, most), 0) == 0, tile, bounds.astype(jnp.int32))


def owned_rows(me, owners, most, parts):
    return pl.pallas_call(
        functools.partial(owner_kernel, parts),
        in_specs=[SMEM, VMEM],
        out_specs=VMEM,
        out_shape=jax.ShapeDtypeStruct((HEAD, most), jnp.int32),
        compiler_params=ROOM,
        name="owned_rows",
    )(me, owners)


def fill_rows(row_ref, moves, start, end, shift):
    unroll = 8

    def one(r):
        at = pl.ds(row_ref[r] - shift, 1)
        for table, rows in moves:
            rows[pl.ds(r, 1), :] = table[at, :]

    def group(i, carry):
        for u in range(unroll):
            one(start + i * unroll + u)
        return carry

    def rest(r, carry):
        one(r)
        return carry

    groups = (end - start) // unroll
    lax.fori_loop(0, groups, group, 0)
    lax.fori_loop(start + groups * unroll, end, rest, 0)


def fill_part(m, sub, me_ref, row_ref, moves):
    most = moves[0][1].shape[0]
    tiles = moves[0][0].shape[0] - HEAD
    at = (me_ref[1] ^ m) * SUBS + sub
    fill_rows(row_ref, moves, row_ref[most + at], row_ref[most + at + 1], at * tiles)


def early_kernel(me_ref, row_ref, *refs):
    pieces, (own_rows, other_rows, flag_ref) = refs[:-3], refs[-3:]
    own, other = pieces[:SUBS], pieces[SUBS:]
    tiles = own[0].shape[0] - HEAD
    flag_ref[0] = jnp.max(own[0][tiles:, :]).astype(jnp.int32)
    own_rows[...] = jnp.zeros_like(own_rows)
    other_rows[...] = jnp.zeros_like(other_rows)
    for sub in range(SUBS):
        fill_part(0, sub, me_ref, row_ref, ((own[sub], own_rows), (other[sub], other_rows)))


def early(me, rows, own, other, most):
    out = jax.ShapeDtypeStruct((most, own[0].shape[1]), jnp.float32)
    return pl.pallas_call(
        early_kernel,
        in_specs=[SMEM, SMEM] + [VMEM] * (2 * SUBS),
        out_specs=[VMEM, VMEM, SMEM],
        out_shape=[out, out, jax.ShapeDtypeStruct((1,), jnp.int32)],
        compiler_params=ROOM,
        name="early",
    )(me, rows, *own, *other)


def middle_kernel(me_ref, row_ref, before_ref, *refs):
    pieces, rows_ref = refs[:-1], refs[-1]
    rows_ref[...] = before_ref[...]
    for i, piece in enumerate(pieces):
        fill_part(1 + i // SUBS, i % SUBS, me_ref, row_ref, ((piece, rows_ref),))


def middle(me, rows, before, pieces):
    return pl.pallas_call(
        middle_kernel,
        in_specs=[SMEM, SMEM, VMEM] + [VMEM] * len(pieces),
        out_specs=VMEM,
        out_shape=jax.ShapeDtypeStruct(before.shape, jnp.float32),
        compiler_params=ROOM,
        name="middle",
    )(me, rows, before, *pieces)


def late_kernel(me_ref, row_ref, own_rows, before_ref, *refs):
    pieces, (owned_ref, map_ref, other_rows) = refs[:-3], refs[-3:]
    tiles, pixels = pieces[0].shape[0] - HEAD, pieces[0].shape[1]
    half = len(pieces) // 2
    lower = me_ref[2] == 0

    def put(ref, at, own, other):
        ref[at, :pixels] = jnp.where(lower, own, other)
        ref[at, pixels:] = jnp.where(lower, other, own)

    other_rows[...] = before_ref[...]
    for i in range(half):
        own, other = pieces[i], pieces[half + i]
        m, sub = i // SUBS, i % SUBS
        at = pl.multiple_of(((me_ref[1] ^ m) * SUBS + sub) * tiles, tiles)
        put(map_ref, pl.ds(at, tiles), own[:tiles, :], other[:tiles, :])
        if m:
            fill_part(m, sub, me_ref, row_ref, ((other, other_rows),))
    put(owned_ref, slice(None), own_rows[...], other_rows[...])


def late(me, rows, own_rows, before, own, other, block):
    most, pixels = own_rows.shape
    return pl.pallas_call(
        late_kernel,
        in_specs=[SMEM, SMEM] + [VMEM] * (2 + len(own) + len(other)),
        out_specs=[VMEM, VMEM],
        out_shape=[
            jax.ShapeDtypeStruct((most, 2 * pixels), jnp.float32),
            jax.ShapeDtypeStruct((block, 2 * pixels), jnp.float32),
        ],
        scratch_shapes=[pltpu.VMEM((most, pixels), jnp.float32)],
        compiler_params=ROOM,
        name="late",
    )(me, rows, own_rows, before, *own, *other)


def shards(kernel, pressure, velocity, entry_slot, slot_tile, tile_owner):
    vols = lax.axis_size("vol")
    pixs = lax.axis_size("pix")
    vol = lax.axis_index("vol")
    pix = lax.axis_index("pix")
    entries, _ = kernel.shape
    slots = slot_tile.shape[1]
    block = tile_owner.shape[0] // vols
    parts = pixs // 2
    part_tiles = block // parts
    half = vols // 2
    most_owned = 2 * block // pixs
    most_rows = min(2 * slots // vols, part_tiles)
    me = jnp.stack([vol, pix >> 1, pix & 1]).astype(jnp.int32)
    tiles = slot_tile.reshape(slots // LANES, LANES)
    slot = entry_slot.reshape(entries // LANES, LANES)
    factors = [x.reshape(entries // LANES, LANES) for x in (pressure, velocity)]
    owners = lax.dynamic_slice_in_dim(
        tile_owner.reshape(vols, block // LANES, LANES), vol, 1
    )[0]
    rows = owned_rows(me, owners, most_owned, parts)[:2].reshape(-1)

    def send(x, vol_step=0, part_step=0, core_step=0):
        step = (vol_step * parts + part_step) * 2 + core_step
        return lax.ppermute(x, ("vol", "pix"), [(d, d ^ step) for d in range(vols * pixs)])

    def exchange(cap, both):
        count = half * parts
        place, ends, head = plan(me, tiles, slot, vols, parts, block, cap, both)
        own, given = project(
            me, kernel, factors, slot, ends.reshape(-1), place.reshape(-1), head, cap
        )
        messages = pack(me, own, send(given, core_step=1), cap, both)

        def gather(messages):
            messages = list(messages)
            for k in reversed(range(1, count)):
                messages[k] = send(messages[k], k // parts, k % parts)
            return collect(messages, part_tiles // SUBS)

        far = gather(messages[count:])
        crossed = [send(x, vol_step=half) for x in far]
        near = gather(messages[:count])
        mine = [x + y for x, y in zip(near, crossed)]
        other = [send(x, core_step=1) for x in mine]
        own_rows, other_rows, flag = early(me, rows, mine, other, most_owned)
        across = [send(x, part_step=m) for m in range(1, parts) for x in mine]
        beyond = [send(x, core_step=1) for x in across]
        own_rows = middle(me, rows, own_rows, across)
        full = late(me, rows, own_rows, other_rows, mine + across, other + beyond, block)
        return flag[0] > 0, *full

    def rows_of(share):
        return most_rows * share // 32 // 8 * 8

    result = exchange(rows_of(13), rows_of(24))

    def redo(state):
        unused, *full = exchange(most_rows, 2 * most_rows)
        return jnp.zeros((), bool), *full

    _, owned, shell = lax.while_loop(lambda state: state[0], redo, result)
    return owned, shell


def solution(mesh):
    in_specs = (
        P(("vol", "pix"), None),
        P(("vol", "pix")),
        P(("vol", "pix")),
        P(("vol", "pix"), None),
        P(("vol", "pix"), None),
        P(),
    )
    out_specs = (P(("vol", "pix"), None), P("vol", None))
    return jax.shard_map(shards, mesh=mesh, in_specs=in_specs, out_specs=out_specs, check_vma=False)
```

profile of v0, /device:TPU:0, one launch (start us, length us, event | category | flops | bytes accessed | tf_op | source)
XLA Modules:
  0.0 58.8 jit_solution(17592207484748965393)
XLA Ops:
  0.7 1.6 %plan.3 = (s32[8,128]{1,0:T(8,128)S(1)}, s32[8,128]{1,0:T(8,128)S(1)}, f32[128,128]{1,0:T(8,128)S(1)}) custom-call(s32[3]{0:T(128)S(1)} %pad_add_fusion.me_ref, s32[8,128]{1,0:T(8,128)} %bitcast.34, s32[128,128]{1,0:T(8,128)} %bitcast.23), custom_call_target="tpu_custom_call" | custom-call | tf_op jit(solution)/shard_map/plan/pallas_call | solution.py:106
  2.3 5.1 %project.3 = (f32[1792,128]{1,0:T(8,128)S(1)}, f32[1792,128]{1,0:T(8,128)S(1)}) custom-call(s32[3]{0:T(128)S(1)} %pad_add_fusion.me_ref, s32[1024]{0:T(1024)S(1)} %bitcast.22, s32[1024]{0:T(1024)S(1)} %bitcast.21, bf16[16384,128]{1,0:T(8,128)(2,1)} %kernel_hbm.1, bf16[128,128]{1,0:T(8,128)(2,1)} %bitcast.30, bf16[128,128]{1,0:T(8,128)(2,1)} %bitcast.32, ...), custom_call_target="tpu_custom_call" | custom-call | tf_op jit(solution)/shard_map/project/pallas_call | solution.py:214
  8.0 2.1 %collective-permute-done.23.other_ref = f32[1792,128]{1,0:T(8,128)S(1)} collective-permute-done((f32[1792,128]{1,0:T(8,128)S(1)}, f32[1792,128]{1,0:T(8,128)S(1)}, u32[]{:S(2)}, u32[]{:S(2)}) %collective-permute-start.23) | collective-permute-done | bytes 917536 | tf_op jit(solution)/shard_map/ppermute | solution.py:473
  10.8 2.9 %collective-permute-start.31 = (f32[200,128]{1,0:T(8,128)S(1)}, f32[200,128]{1,0:T(8,128)S(1)}, u32[]{:S(2)}, u32[]{:S(2)}) collective-permute-start(f32[200,128]{1,0:T(8,128)S(1)} %get-tuple-element.126), channel_id=1, source_target_pairs={{0,2},{1,3},{2,0},{3,1},{4,6},{5,7},{6,4},{7,5},{8,10},{9,11},{10,... | collective-permute-start | bytes 307208 | tf_op jit(solution)/shard_map/ppermute | solution.py:473
  13.7 1.5 %collective-permute-start.32 = (f32[200,128]{1,0:T(8,128)S(1)}, f32[200,128]{1,0:T(8,128)S(1)}, u32[]{:S(2)}, u32[]{:S(2)}) collective-permute-start(f32[200,128]{1,0:T(8,128)S(1)} %get-tuple-element.127), channel_id=1, source_target_pairs={{0,4},{1,5},{2,6},{3,7},{4,0},{5,1},{6,2},{7,3},{8,12},{9,13},{10,... | collective-permute-start | bytes 307208 | tf_op jit(solution)/shard_map/ppermute | solution.py:473
  15.3 2.0 %collective-permute-start.34 = (f32[200,128]{1,0:T(8,128)S(1)}, f32[200,128]{1,0:T(8,128)S(1)}, u32[]{:S(2)}, u32[]{:S(2)}) collective-permute-start(f32[200,128]{1,0:T(8,128)S(1)} %get-tuple-element.129), channel_id=1, source_target_pairs={{0,8},{1,9},{2,10},{3,11},{4,12},{5,13},{6,14},{7,15},{8,0},{9,1},... | collective-permute-start | bytes 307208 | tf_op jit(solution)/shard_map/ppermute | solution.py:473
  17.3 1.4 %collective-permute-start.35 = (f32[200,128]{1,0:T(8,128)S(1)}, f32[200,128]{1,0:T(8,128)S(1)}, u32[]{:S(2)}, u32[]{:S(2)}) collective-permute-start(f32[200,128]{1,0:T(8,128)S(1)} %get-tuple-element.130), channel_id=1, source_target_pairs={{0,10},{1,11},{2,8},{3,9},{4,14},{5,15},{6,12},{7,13},{8,2},{9,3},... | collective-permute-start | bytes 307208 | tf_op jit(solution)/shard_map/ppermute | solution.py:473
  18.7 2.5 %collective-permute-start.36 = (f32[200,128]{1,0:T(8,128)S(1)}, f32[200,128]{1,0:T(8,128)S(1)}, u32[]{:S(2)}, u32[]{:S(2)}) collective-permute-start(f32[200,128]{1,0:T(8,128)S(1)} %get-tuple-element.131), channel_id=1, source_target_pairs={{0,12},{1,13},{2,14},{3,15},{4,8},{5,9},{6,10},{7,11},{8,4},{9,5},... | collective-permute-start | bytes 307208 | tf_op jit(solution)/shard_map/ppermute | solution.py:473
  21.2 1.3 %collective-permute-start.37 = (f32[200,128]{1,0:T(8,128)S(1)}, f32[200,128]{1,0:T(8,128)S(1)}, u32[]{:S(2)}, u32[]{:S(2)}) collective-permute-start(f32[200,128]{1,0:T(8,128)S(1)} %get-tuple-element.132), channel_id=1, source_target_pairs={{0,14},{1,15},{2,12},{3,13},{4,10},{5,11},{6,8},{7,9},{8,6},{9,7},... | collective-permute-start | bytes 307208 | tf_op jit(solution)/shard_map/ppermute | solution.py:473
  22.5 2.1 %collective-permute-start.24 = (f32[200,128]{1,0:T(8,128)S(1)}, f32[200,128]{1,0:T(8,128)S(1)}, u32[]{:S(2)}, u32[]{:S(2)}) collective-permute-start(f32[200,128]{1,0:T(8,128)S(1)} %get-tuple-element.117), channel_id=1, source_target_pairs={{0,2},{1,3},{2,0},{3,1},{4,6},{5,7},{6,4},{7,5},{8,10},{9,11},{10,... | collective-permute-start | bytes 307208 | tf_op jit(solution)/shard_map/ppermute | solution.py:473
  24.7 1.8 %collective-permute-start.26 = (f32[200,128]{1,0:T(8,128)S(1)}, f32[200,128]{1,0:T(8,128)S(1)}, u32[]{:S(2)}, u32[]{:S(2)}) collective-permute-start(f32[200,128]{1,0:T(8,128)S(1)} %get-tuple-element.119), channel_id=1, source_target_pairs={{0,6},{1,7},{2,4},{3,5},{4,2},{5,3},{6,0},{7,1},{8,14},{9,15},{10,... | collective-permute-start | bytes 307208 | tf_op jit(solution)/shard_map/ppermute | solution.py:473
  28.3 1.2 %collective-permute-done.37.refs_7_ = f32[200,128]{1,0:T(8,128)S(1)} collective-permute-done((f32[200,128]{1,0:T(8,128)S(1)}, f32[200,128]{1,0:T(8,128)S(1)}, u32[]{:S(2)}, u32[]{:S(2)}) %collective-permute-start.37) | collective-permute-done | bytes 102432 | tf_op jit(solution)/shard_map/ppermute | solution.py:473
  30.2 2.6 %collective-permute-start.39 = (f32[264,128]{1,0:T(8,128)S(1)}, f32[264,128]{1,0:T(8,128)S(1)}, u32[]{:S(2)}, u32[]{:S(2)}) collective-permute-start(f32[264,128]{1,0:T(8,128)S(1)} %get-tuple-element.135), channel_id=1, source_target_pairs={{0,16},{1,17},{2,18},{3,19},{4,20},{5,21},{6,22},{7,23},{8,24},{9,... | collective-permute-start | bytes 405512 | tf_op jit(solution)/shard_map/ppermute | solution.py:473
  33.2 1.1 %collective-permute-start.28 = (f32[200,128]{1,0:T(8,128)S(1)}, f32[200,128]{1,0:T(8,128)S(1)}, u32[]{:S(2)}, u32[]{:S(2)}) collective-permute-start(f32[200,128]{1,0:T(8,128)S(1)} %get-tuple-element.121), channel_id=1, source_target_pairs={{0,10},{1,11},{2,8},{3,9},{4,14},{5,15},{6,12},{7,13},{8,2},{9,3},... | collective-permute-start | bytes 307208 | tf_op jit(solution)/shard_map/ppermute | solution.py:473
  35.2 3.5 %collective-permute-start.30 = (f32[200,128]{1,0:T(8,128)S(1)}, f32[200,128]{1,0:T(8,128)S(1)}, u32[]{:S(2)}, u32[]{:S(2)}) collective-permute-start(f32[200,128]{1,0:T(8,128)S(1)} %get-tuple-element.123), channel_id=1, source_target_pairs={{0,14},{1,15},{2,12},{3,13},{4,10},{5,11},{6,8},{7,9},{8,6},{9,7},... | collective-permute-start | bytes 307208 | tf_op jit(solution)/shard_map/ppermute | solution.py:473
  38.6 5.2 %collective-permute-done.28.refs_5_ = f32[200,128]{1,0:T(8,128)S(1)} collective-permute-done((f32[200,128]{1,0:T(8,128)S(1)}, f32[200,128]{1,0:T(8,128)S(1)}, u32[]{:S(2)}, u32[]{:S(2)}) %collective-permute-start.28) | collective-permute-done | bytes 102432 | tf_op jit(solution)/shard_map/ppermute | solution.py:473
  44.8 1.2 %collective-permute-done.30.refs_7_ = f32[200,128]{1,0:T(8,128)S(1)} collective-permute-done((f32[200,128]{1,0:T(8,128)S(1)}, f32[200,128]{1,0:T(8,128)S(1)}, u32[]{:S(2)}, u32[]{:S(2)}) %collective-permute-start.30) | collective-permute-done | bytes 102432 | tf_op jit(solution)/shard_map/ppermute | solution.py:473
  46.8 1.1 %collective-permute-start.43 = (f32[264,128]{1,0:T(8,128)S(1)}, f32[264,128]{1,0:T(8,128)S(1)}, u32[]{:S(2)}, u32[]{:S(2)}) collective-permute-start(f32[264,128]{1,0:T(8,128)S(1)} %add.17.refs_1_), channel_id=1, source_target_pairs={{0,2},{1,3},{2,0},{3,1},{4,6},{5,7},{6,4},{7,5},{8,10},{9,11},{10,... | collective-permute-start | bytes 405512 | tf_op jit(solution)/shard_map/ppermute | solution.py:473
  47.9 1.0 %collective-permute-start.42 = (f32[264,128]{1,0:T(8,128)S(1)}, f32[264,128]{1,0:T(8,128)S(1)}, u32[]{:S(2)}, u32[]{:S(2)}) collective-permute-start(f32[264,128]{1,0:T(8,128)S(1)} %add.16.refs_0_), channel_id=1, source_target_pairs={{0,2},{1,3},{2,0},{3,1},{4,6},{5,7},{6,4},{7,5},{8,10},{9,11},{10,... | collective-permute-start | bytes 405512 | tf_op jit(solution)/shard_map/ppermute | solution.py:473
  49.0 1.2 %owned_rows.1 = s32[8,512]{1,0:T(8,128)S(1)} custom-call(s32[3]{0:T(128)S(1)} %pad_add_fusion.me_ref, s32[8,128]{1,0:T(8,128)S(1)} %dynamic-slice_bitcast_fusion.owner_ref), custom_call_target="tpu_custom_call" | custom-call | tf_op jit(solution)/shard_map/owned_rows/pallas_call | solution.py:332
  50.7 1.6 %collective-permute-done.43.refs_1_.refs_3_ = f32[264,128]{1,0:T(8,128)S(1)} collective-permute-done((f32[264,128]{1,0:T(8,128)S(1)}, f32[264,128]{1,0:T(8,128)S(1)}, u32[]{:S(2)}, u32[]{:S(2)}) %collective-permute-start.43) | collective-permute-done | bytes 135200 | tf_op jit(solution)/shard_map/ppermute | solution.py:473
  52.3 1.4 %collective-permute-done.42.refs_0_.refs_2_ = f32[264,128]{1,0:T(8,128)S(1)} collective-permute-done((f32[264,128]{1,0:T(8,128)S(1)}, f32[264,128]{1,0:T(8,128)S(1)}, u32[]{:S(2)}, u32[]{:S(2)}) %collective-permute-start.42) | collective-permute-done | bytes 135200 | tf_op jit(solution)/shard_map/ppermute | solution.py:473
  53.8 1.5 %early.3 = (f32[512,128]{1,0:T(8,128)S(1)}, f32[512,128]{1,0:T(8,128)S(1)}, s32[1]{0:T(128)}) custom-call(s32[3]{0:T(128)S(1)} %pad_add_fusion.me_ref, s32[1024]{0:T(1024)S(1)} %bitcast.26, f32[264,128]{1,0:T(8,128)S(1)} %add.16.refs_0_, f32[264,128]{1,0:T(8,128)S(1)} %add.17.refs_1_, f32[264,128]{1,0:T(8,128)S(1)} %collective-permute-done.40.refs_2_.refs_4_, ...), custom_call_target="tpu_custom_call" | custom-call | tf_op jit(solution)/shard_map/early/pallas_call | solution.py:384
  56.7 2.0 %late.3 = (f32[512,256]{1,0:T(8,128)}, f32[1024,256]{1,0:T(8,128)}) custom-call(s32[3]{0:T(128)S(1)} %pad_add_fusion.me_ref, s32[1024]{0:T(1024)S(1)} %bitcast.28, f32[512,128]{1,0:T(8,128)S(1)} %middle.3.own_rows, f32[512,128]{1,0:T(8,128)S(1)} %get-tuple-element.138.before_ref, f32[264,128]{1,0:T(8,128)S(1)} %add.16.refs_0_, f32[264,128]{1,0:T(8,128)S(1)} %add.17.refs_1_, ...), custom_call_target="tpu_custom_call" | custom-call | tf_op jit(solution)/shard_map/late/pallas_call | solution.py:435
  (48 shorter events, 8.3 us)
Async XLA Ops:
  0.6 48.3 %copy-start = (s32[8192]{0:T(1024)S(1)}, s32[8192]{0:T(1024)}, u32[]{:S(2)}) copy-start(s32[8192]{0:T(1024)} %param.13) | copy-start | bytes 98308
  7.5 2.7 %collective-permute-start.23 = (f32[1792,128]{1,0:T(8,128)S(1)}, f32[1792,128]{1,0:T(8,128)S(1)}, u32[]{:S(2)}, u32[]{:S(2)}) collective-permute-start(f32[1792,128]{1,0:T(8,128)S(1)} %get-tuple-element.115), channel_id=1, source_target_pairs={{0,1},{1,0},{2,3},{3,2},{4,5},{5,4},{6,7},{7,6},{8,9},{9,8},{10,11... | collective-permute-start | bytes 2752520 | tf_op jit(solution)/shard_map/ppermute | solution.py:473
  10.8 7.9 %collective-permute-start.31 = (f32[200,128]{1,0:T(8,128)S(1)}, f32[200,128]{1,0:T(8,128)S(1)}, u32[]{:S(2)}, u32[]{:S(2)}) collective-permute-start(f32[200,128]{1,0:T(8,128)S(1)} %get-tuple-element.126), channel_id=1, source_target_pairs={{0,2},{1,3},{2,0},{3,1},{4,6},{5,7},{6,4},{7,5},{8,10},{9,11},{10,... | collective-permute-start | bytes 307208 | tf_op jit(solution)/shard_map/ppermute | solution.py:473
  13.7 7.5 %collective-permute-start.32 = (f32[200,128]{1,0:T(8,128)S(1)}, f32[200,128]{1,0:T(8,128)S(1)}, u32[]{:S(2)}, u32[]{:S(2)}) collective-permute-start(f32[200,128]{1,0:T(8,128)S(1)} %get-tuple-element.127), channel_id=1, source_target_pairs={{0,4},{1,5},{2,6},{3,7},{4,0},{5,1},{6,2},{7,3},{8,12},{9,13},{10,... | collective-permute-start | bytes 307208 | tf_op jit(solution)/shard_map/ppermute | solution.py:473
  15.2 7.3 %collective-permute-start.33 = (f32[200,128]{1,0:T(8,128)S(1)}, f32[200,128]{1,0:T(8,128)S(1)}, u32[]{:S(2)}, u32[]{:S(2)}) collective-permute-start(f32[200,128]{1,0:T(8,128)S(1)} %get-tuple-element.128), channel_id=1, source_target_pairs={{0,6},{1,7},{2,4},{3,5},{4,2},{5,3},{6,0},{7,1},{8,14},{9,15},{10,... | collective-permute-start | bytes 307208 | tf_op jit(solution)/shard_map/ppermute | solution.py:473
  15.3 9.3 %collective-permute-start.34 = (f32[200,128]{1,0:T(8,128)S(1)}, f32[200,128]{1,0:T(8,128)S(1)}, u32[]{:S(2)}, u32[]{:S(2)}) collective-permute-start(f32[200,128]{1,0:T(8,128)S(1)} %get-tuple-element.129), channel_id=1, source_target_pairs={{0,8},{1,9},{2,10},{3,11},{4,12},{5,13},{6,14},{7,15},{8,0},{9,1},... | collective-permute-start | bytes 307208 | tf_op jit(solution)/shard_map/ppermute | solution.py:473
  17.3 7.4 %collective-permute-start.35 = (f32[200,128]{1,0:T(8,128)S(1)}, f32[200,128]{1,0:T(8,128)S(1)}, u32[]{:S(2)}, u32[]{:S(2)}) collective-permute-start(f32[200,128]{1,0:T(8,128)S(1)} %get-tuple-element.130), channel_id=1, source_target_pairs={{0,10},{1,11},{2,8},{3,9},{4,14},{5,15},{6,12},{7,13},{8,2},{9,3},... | collective-permute-start | bytes 307208 | tf_op jit(solution)/shard_map/ppermute | solution.py:473
  18.7 8.8 %collective-permute-start.36 = (f32[200,128]{1,0:T(8,128)S(1)}, f32[200,128]{1,0:T(8,128)S(1)}, u32[]{:S(2)}, u32[]{:S(2)}) collective-permute-start(f32[200,128]{1,0:T(8,128)S(1)} %get-tuple-element.131), channel_id=1, source_target_pairs={{0,12},{1,13},{2,14},{3,15},{4,8},{5,9},{6,10},{7,11},{8,4},{9,5},... | collective-permute-start | bytes 307208 | tf_op jit(solution)/shard_map/ppermute | solution.py:473
  21.2 8.3 %collective-permute-start.37 = (f32[200,128]{1,0:T(8,128)S(1)}, f32[200,128]{1,0:T(8,128)S(1)}, u32[]{:S(2)}, u32[]{:S(2)}) collective-permute-start(f32[200,128]{1,0:T(8,128)S(1)} %get-tuple-element.132), channel_id=1, source_target_pairs={{0,14},{1,15},{2,12},{3,13},{4,10},{5,11},{6,8},{7,9},{8,6},{9,7},... | collective-permute-start | bytes 307208 | tf_op jit(solution)/shard_map/ppermute | solution.py:473
  22.5 10.3 %collective-permute-start.24 = (f32[200,128]{1,0:T(8,128)S(1)}, f32[200,128]{1,0:T(8,128)S(1)}, u32[]{:S(2)}, u32[]{:S(2)}) collective-permute-start(f32[200,128]{1,0:T(8,128)S(1)} %get-tuple-element.117), channel_id=1, source_target_pairs={{0,2},{1,3},{2,0},{3,1},{4,6},{5,7},{6,4},{7,5},{8,10},{9,11},{10,... | collective-permute-start | bytes 307208 | tf_op jit(solution)/shard_map/ppermute | solution.py:473
  24.6 8.6 %collective-permute-start.25 = (f32[200,128]{1,0:T(8,128)S(1)}, f32[200,128]{1,0:T(8,128)S(1)}, u32[]{:S(2)}, u32[]{:S(2)}) collective-permute-start(f32[200,128]{1,0:T(8,128)S(1)} %get-tuple-element.118), channel_id=1, source_target_pairs={{0,4},{1,5},{2,6},{3,7},{4,0},{5,1},{6,2},{7,3},{8,12},{9,13},{10,... | collective-permute-start | bytes 307208 | tf_op jit(solution)/shard_map/ppermute | solution.py:473
  24.7 9.6 %collective-permute-start.26 = (f32[200,128]{1,0:T(8,128)S(1)}, f32[200,128]{1,0:T(8,128)S(1)}, u32[]{:S(2)}, u32[]{:S(2)}) collective-permute-start(f32[200,128]{1,0:T(8,128)S(1)} %get-tuple-element.119), channel_id=1, source_target_pairs={{0,6},{1,7},{2,4},{3,5},{4,2},{5,3},{6,0},{7,1},{8,14},{9,15},{10,... | collective-permute-start | bytes 307208 | tf_op jit(solution)/shard_map/ppermute | solution.py:473
  27.5 7.7 %collective-permute-start.27 = (f32[200,128]{1,0:T(8,128)S(1)}, f32[200,128]{1,0:T(8,128)S(1)}, u32[]{:S(2)}, u32[]{:S(2)}) collective-permute-start(f32[200,128]{1,0:T(8,128)S(1)} %get-tuple-element.120), channel_id=1, source_target_pairs={{0,8},{1,9},{2,10},{3,11},{4,12},{5,13},{6,14},{7,15},{8,0},{9,1},... | collective-permute-start | bytes 307208 | tf_op jit(solution)/shard_map/ppermute | solution.py:473
  30.2 16.5 %collective-permute-start.39 = (f32[264,128]{1,0:T(8,128)S(1)}, f32[264,128]{1,0:T(8,128)S(1)}, u32[]{:S(2)}, u32[]{:S(2)}) collective-permute-start(f32[264,128]{1,0:T(8,128)S(1)} %get-tuple-element.135), channel_id=1, source_target_pairs={{0,16},{1,17},{2,18},{3,19},{4,20},{5,21},{6,22},{7,23},{8,24},{9,... | collective-permute-start | bytes 405512 | tf_op jit(solution)/shard_map/ppermute | solution.py:473
  32.9 15.0 %collective-permute-start.38 = (f32[264,128]{1,0:T(8,128)S(1)}, f32[264,128]{1,0:T(8,128)S(1)}, u32[]{:S(2)}, u32[]{:S(2)}) collective-permute-start(f32[264,128]{1,0:T(8,128)S(1)} %get-tuple-element.133), channel_id=1, source_target_pairs={{0,16},{1,17},{2,18},{3,19},{4,20},{5,21},{6,22},{7,23},{8,24},{9,... | collective-permute-start | bytes 405512 | tf_op jit(solution)/shard_map/ppermute | solution.py:473
  33.2 10.6 %collective-permute-start.28 = (f32[200,128]{1,0:T(8,128)S(1)}, f32[200,128]{1,0:T(8,128)S(1)}, u32[]{:S(2)}, u32[]{:S(2)}) collective-permute-start(f32[200,128]{1,0:T(8,128)S(1)} %get-tuple-element.121), channel_id=1, source_target_pairs={{0,10},{1,11},{2,8},{3,9},{4,14},{5,15},{6,12},{7,13},{8,2},{9,3},... | collective-permute-start | bytes 307208 | tf_op jit(solution)/shard_map/ppermute | solution.py:473
  34.3 10.5 %collective-permute-start.29 = (f32[200,128]{1,0:T(8,128)S(1)}, f32[200,128]{1,0:T(8,128)S(1)}, u32[]{:S(2)}, u32[]{:S(2)}) collective-permute-start(f32[200,128]{1,0:T(8,128)S(1)} %get-tuple-element.122), channel_id=1, source_target_pairs={{0,12},{1,13},{2,14},{3,15},{4,8},{5,9},{6,10},{7,11},{8,4},{9,5},... | collective-permute-start | bytes 307208 | tf_op jit(solution)/shard_map/ppermute | solution.py:473
  35.2 10.8 %collective-permute-start.30 = (f32[200,128]{1,0:T(8,128)S(1)}, f32[200,128]{1,0:T(8,128)S(1)}, u32[]{:S(2)}, u32[]{:S(2)}) collective-permute-start(f32[200,128]{1,0:T(8,128)S(1)} %get-tuple-element.123), channel_id=1, source_target_pairs={{0,14},{1,15},{2,12},{3,13},{4,10},{5,11},{6,8},{7,9},{8,6},{9,7},... | collective-permute-start | bytes 307208 | tf_op jit(solution)/shard_map/ppermute | solution.py:473
  46.8 5.5 %collective-permute-start.43 = (f32[264,128]{1,0:T(8,128)S(1)}, f32[264,128]{1,0:T(8,128)S(1)}, u32[]{:S(2)}, u32[]{:S(2)}) collective-permute-start(f32[264,128]{1,0:T(8,128)S(1)} %add.17.refs_1_), channel_id=1, source_target_pairs={{0,2},{1,3},{2,0},{3,1},{4,6},{5,7},{6,4},{7,5},{8,10},{9,11},{10,... | collective-permute-start | bytes 405512 | tf_op jit(solution)/shard_map/ppermute | solution.py:473
  47.9 5.8 %collective-permute-start.42 = (f32[264,128]{1,0:T(8,128)S(1)}, f32[264,128]{1,0:T(8,128)S(1)}, u32[]{:S(2)}, u32[]{:S(2)}) collective-permute-start(f32[264,128]{1,0:T(8,128)S(1)} %add.16.refs_0_), channel_id=1, source_target_pairs={{0,2},{1,3},{2,0},{3,1},{4,6},{5,7},{6,4},{7,5},{8,10},{9,11},{10,... | collective-permute-start | bytes 405512 | tf_op jit(solution)/shard_map/ppermute | solution.py:473
  50.1 3.6 %collective-permute-start.41 = (f32[264,128]{1,0:T(8,128)S(1)}, f32[264,128]{1,0:T(8,128)S(1)}, u32[]{:S(2)}, u32[]{:S(2)}) collective-permute-start(f32[264,128]{1,0:T(8,128)S(1)} %add.17.refs_1_), channel_id=1, source_target_pairs={{0,1},{1,0},{2,3},{3,2},{4,5},{5,4},{6,7},{7,6},{8,9},{9,8},{10,11... | collective-permute-start | bytes 405512 | tf_op jit(solution)/shard_map/ppermute | solution.py:473
  50.2 3.5 %collective-permute-start.40 = (f32[264,128]{1,0:T(8,128)S(1)}, f32[264,128]{1,0:T(8,128)S(1)}, u32[]{:S(2)}, u32[]{:S(2)}) collective-permute-start(f32[264,128]{1,0:T(8,128)S(1)} %add.16.refs_0_), channel_id=1, source_target_pairs={{0,1},{1,0},{2,3},{3,2},{4,5},{5,4},{6,7},{7,6},{8,9},{9,8},{10,11... | collective-permute-start | bytes 405512 | tf_op jit(solution)/shard_map/ppermute | solution.py:473
  52.3 4.4 %collective-permute-start.45 = (f32[264,128]{1,0:T(8,128)S(1)}, f32[264,128]{1,0:T(8,128)S(1)}, u32[]{:S(2)}, u32[]{:S(2)}) collective-permute-start(f32[264,128]{1,0:T(8,128)S(1)} %collective-permute-done.43.refs_1_.refs_3_), channel_id=1, source_target_pairs={{0,1},{1,0},{2,3},{3,2},{4,5},{5,4},{6,7},{7,6},{8,9},{9,8},{10,11... | collective-permute-start | bytes 405512 | tf_op jit(solution)/shard_map/ppermute | solution.py:473
  53.7 3.0 %collective-permute-start.44 = (f32[264,128]{1,0:T(8,128)S(1)}, f32[264,128]{1,0:T(8,128)S(1)}, u32[]{:S(2)}, u32[]{:S(2)}) collective-permute-start(f32[264,128]{1,0:T(8,128)S(1)} %collective-permute-done.42.refs_0_.refs_2_), channel_id=1, source_target_pairs={{0,1},{1,0},{2,3},{3,2},{4,5},{5,4},{6,7},{7,6},{8,9},{9,8},{10,11... | collective-permute-start | bytes 405512 | tf_op jit(solution)/shard_map/ppermute | solution.py:473
  (4 other events, 51.1 us)
where the time goes:
time: 60 us; the launch traced here: 58.8 us
  starting transfers between devices  28.1 us (47%)
  waiting for transfers between devices  14.8 us (25%)
  Pallas kernels  14.3 us (24%)
  between operations  1.43 us (2%)
    ppermute x23, starting transfers between devices, send(): lax.ppermute(x, ('vol', 'pix'), [(d, d ^ step) for d in range(vols * pixs)])  28.1 us
    ppermute x23, waiting for transfers between devices, send(): lax.ppermute(x, ('vol', 'pix'), [(d, d ^ step) for d in range(vols * pixs)])  14.8 us
    pallas_call x1, Pallas kernels, project(): pl.pallas_call(functools.partial(project_kernel, steps, cap), in_specs=[S...  5.14 us
    pallas_call x1, Pallas kernels, late(): pl.pallas_call(late_kernel, in_specs=[SMEM, SMEM] + [VMEM] * (2 + len(own...  2.05 us
    pallas_call x1, Pallas kernels, plan(): pl.pallas_call(functools.partial(plan_kernel, vols, parts, block, cap, bo...  1.59 us
    pallas_call x1, Pallas kernels, early(): pl.pallas_call(early_kernel, in_specs=[SMEM, SMEM] + [VMEM] * (2 * SUBS),...  1.47 us
    pallas_call x2, Pallas kernels, collect(): pl.pallas_call(functools.partial(collect_kernel, len(messages), sub_tiles...  1.43 us
  transfers between devices with their start and end apart: 23, of which 9 were waited for; matrix products, arithmetic and copies ran while one was open for 0% of the time, Pallas kernels for 8%

commit v1 on v0

--- a/solution.py
+++ b/solution.py
@@ -77,7 +77,7 @@
     fits = place < cap
     spilled = jnp.sum(jnp.where(fits, 0.0, 1.0), axis=(0, 1), keepdims=True)
     place = jnp.where(me_ref[2] == 0, place, cap - 1 - place)
-    place_ref[...] = jnp.where(fits, group * size + place, classes * size)
+    place_ref[...] = jnp.where(fits, group * size + place, classes * size - 1)
     lists = -(-both // LANES)
     width = lists * LANES
     spot = jnp.where(fits, place + me_ref[2] * (both - cap), -1)
@@ -120,7 +120,7 @@
 def project_kernel(
     steps, cap, me_ref, ends_ref, place_ref, kernel_hbm, thermal_ref, kinetic_ref, slot_ref, head_ref,
     own_out, other_out,
-    kernel_ref, own_ref, other_ref, own_stage, other_stage, own_s, other_s, in_sem
+    kernel_ref, own_ref, other_ref, own_s, other_s, in_sem
 ):
     entries, _ = kernel_ref.shape
     part = entries // steps
@@ -135,7 +135,7 @@
 
     for step in range(steps):
         load(step).start()
-    for ref in (own_ref, other_ref, own_stage, other_stage):
+    for ref in (own_ref, other_ref, own_out, other_out):
         ref[...] = jnp.zeros_like(ref)
     thermal, kinetic = thermal_ref[...].astype(jnp.float32), kinetic_ref[...].astype(jnp.float32)
     own_s[...] = jnp.where(me_ref[2] == 0, thermal, kinetic)
@@ -190,16 +190,15 @@
         for u in range(unroll):
             s = i * unroll + u
             to = place_ref[s]
-            own_stage[pl.ds(to, 1), :] = own_ref[pl.ds(s, 1), :]
-            other_stage[pl.ds(to, 1), :] = other_ref[pl.ds(s, 1), :]
+            own_out[pl.ds(to, 1), :] = own_ref[pl.ds(s, 1), :]
+            other_out[pl.ds(to, 1), :] = other_ref[pl.ds(s, 1), :]
         return carry
 
     lax.fori_loop(0, slots // unroll, move, 0)
     size = cap + HEAD
-    for out, stage in ((own_out, own_stage), (other_out, other_stage)):
+    for out in (own_out, other_out):
         for k in range(head_ref.shape[0] // HEAD):
             at = k * size
-            out[at : at + cap, :] = stage[at : at + cap, :]
             out[at + cap : at + size, :] = head_ref[k * HEAD : (k + 1) * HEAD, :]
 
 
@@ -209,7 +208,6 @@
     steps = 4
     rows = head.shape[0] // HEAD * (cap + HEAD)
     partial = pltpu.VMEM((slots + WINDOW, pixels), jnp.float32)
-    stage = pltpu.VMEM((rows + HEAD, pixels), jnp.float32)
     factor = pltpu.VMEM(slot.shape, jnp.float32)
     return pl.pallas_call(
         functools.partial(project_kernel, steps, cap),
@@ -218,7 +216,7 @@
         out_shape=[jax.ShapeDtypeStruct((rows, pixels), jnp.float32)] * 2,
         scratch_shapes=[
             pltpu.VMEM((entries, pixels), kernel.dtype),
-            partial, partial, stage, stage, factor, factor,
+            partial, partial, factor, factor,
             pltpu.SemaphoreType.DMA((steps,)),
         ],
         compiler_params=ROOM,

time: 60 us -> 60 us (level)
  no operation moved by 1% of the time
where the time goes in v1:
time: 60 us; the launch traced here: 58.8 us
  starting transfers between devices  28.1 us (47%)
  waiting for transfers between devices  14.8 us (25%)
  Pallas kernels  14.4 us (24%)
  between operations  1.43 us (2%)
    ppermute x23, starting transfers between devices, send(): lax.ppermute(x, ('vol', 'pix'), [(d, d ^ step) for d in range(vols * pixs)])  28.1 us
    ppermute x23, waiting for transfers between devices, send(): lax.ppermute(x, ('vol', 'pix'), [(d, d ^ step) for d in range(vols * pixs)])  14.8 us
    pallas_call x1, Pallas kernels, project(): pl.pallas_call(functools.partial(project_kernel, steps, cap), in_specs=[S...  5.15 us
    pallas_call x1, Pallas kernels, late(): pl.pallas_call(late_kernel, in_specs=[SMEM, SMEM] + [VMEM] * (2 + len(own...  2.05 us
    pallas_call x1, Pallas kernels, plan(): pl.pallas_call(functools.partial(plan_kernel, vols, parts, block, cap, bo...  1.59 us
    pallas_call x1, Pallas kernels, early(): pl.pallas_call(early_kernel, in_specs=[SMEM, SMEM] + [VMEM] * (2 * SUBS),...  1.47 us
    pallas_call x2, Pallas kernels, collect(): pl.pallas_call(functools.partial(collect_kernel, len(messages), sub_tiles...  1.43 us
  transfers between devices with their start and end apart: 23, of which 9 were waited for; matrix products, arithmetic and copies ran while one was open for 0% of the time, Pallas kernels for 8%

profile of v1, /device:TPU:0, one launch (start us, length us, event | category | flops | bytes accessed | tf_op | source)
XLA Modules:
  0.0 58.8 jit_solution(9698851845697718159)
XLA Ops:
  0.7 1.6 %plan.3 = (s32[8,128]{1,0:T(8,128)S(1)}, s32[8,128]{1,0:T(8,128)S(1)}, f32[128,128]{1,0:T(8,128)S(1)}) custom-call(s32[3]{0:T(128)S(1)} %pad_add_fusion.me_ref, s32[8,128]{1,0:T(8,128)} %bitcast.34, s32[128,128]{1,0:T(8,128)} %bitcast.23), custom_call_target="tpu_custom_call" | custom-call | tf_op jit(solution)/shard_map/plan/pallas_call | solution.py:106
  2.3 5.1 %project.3 = (f32[1792,128]{1,0:T(8,128)S(1)}, f32[1792,128]{1,0:T(8,128)S(1)}) custom-call(s32[3]{0:T(128)S(1)} %pad_add_fusion.me_ref, s32[1024]{0:T(1024)S(1)} %bitcast.22, s32[1024]{0:T(1024)S(1)} %bitcast.21, bf16[16384,128]{1,0:T(8,128)(2,1)} %kernel_hbm.1, bf16[128,128]{1,0:T(8,128)(2,1)} %bitcast.30, bf16[128,128]{1,0:T(8,128)(2,1)} %bitcast.32, ...), custom_call_target="tpu_custom_call" | custom-call | tf_op jit(solution)/shard_map/project/pallas_call | solution.py:212
  8.0 2.1 %collective-permute-done.23.other_ref = f32[1792,128]{1,0:T(8,128)S(1)} collective-permute-done((f32[1792,128]{1,0:T(8,128)S(1)}, f32[1792,128]{1,0:T(8,128)S(1)}, u32[]{:S(2)}, u32[]{:S(2)}) %collective-permute-start.23) | collective-permute-done | bytes 917536 | tf_op jit(solution)/shard_map/ppermute | solution.py:471
  10.8 2.9 %collective-permute-start.31 = (f32[200,128]{1,0:T(8,128)S(1)}, f32[200,128]{1,0:T(8,128)S(1)}, u32[]{:S(2)}, u32[]{:S(2)}) collective-permute-start(f32[200,128]{1,0:T(8,128)S(1)} %get-tuple-element.126), channel_id=1, source_target_pairs={{0,2},{1,3},{2,0},{3,1},{4,6},{5,7},{6,4},{7,5},{8,10},{9,11},{10,... | collective-permute-start | bytes 307208 | tf_op jit(solution)/shard_map/ppermute | solution.py:471
  13.7 1.5 %collective-permute-start.32 = (f32[200,128]{1,0:T(8,128)S(1)}, f32[200,128]{1,0:T(8,128)S(1)}, u32[]{:S(2)}, u32[]{:S(2)}) collective-permute-start(f32[200,128]{1,0:T(8,128)S(1)} %get-tuple-element.127), channel_id=1, source_target_pairs={{0,4},{1,5},{2,6},{3,7},{4,0},{5,1},{6,2},{7,3},{8,12},{9,13},{10,... | collective-permute-start | bytes 307208 | tf_op jit(solution)/shard_map/ppermute | solution.py:471
  15.3 2.0 %collective-permute-start.34 = (f32[200,128]{1,0:T(8,128)S(1)}, f32[200,128]{1,0:T(8,128)S(1)}, u32[]{:S(2)}, u32[]{:S(2)}) collective-permute-start(f32[200,128]{1,0:T(8,128)S(1)} %get-tuple-element.129), channel_id=1, source_target_pairs={{0,8},{1,9},{2,10},{3,11},{4,12},{5,13},{6,14},{7,15},{8,0},{9,1},... | collective-permute-start | bytes 307208 | tf_op jit(solution)/shard_map/ppermute | solution.py:471
  17.3 1.4 %collective-permute-start.35 = (f32[200,128]{1,0:T(8,128)S(1)}, f32[200,128]{1,0:T(8,128)S(1)}, u32[]{:S(2)}, u32[]{:S(2)}) collective-permute-start(f32[200,128]{1,0:T(8,128)S(1)} %get-tuple-element.130), channel_id=1, source_target_pairs={{0,10},{1,11},{2,8},{3,9},{4,14},{5,15},{6,12},{7,13},{8,2},{9,3},... | collective-permute-start | bytes 307208 | tf_op jit(solution)/shard_map/ppermute | solution.py:471
  18.7 2.5 %collective-permute-start.36 = (f32[200,128]{1,0:T(8,128)S(1)}, f32[200,128]{1,0:T(8,128)S(1)}, u32[]{:S(2)}, u32[]{:S(2)}) collective-permute-start(f32[200,128]{1,0:T(8,128)S(1)} %get-tuple-element.131), channel_id=1, source_target_pairs={{0,12},{1,13},{2,14},{3,15},{4,8},{5,9},{6,10},{7,11},{8,4},{9,5},... | collective-permute-start | bytes 307208 | tf_op jit(solution)/shard_map/ppermute | solution.py:471
  21.2 1.3 %collective-permute-start.37 = (f32[200,128]{1,0:T(8,128)S(1)}, f32[200,128]{1,0:T(8,128)S(1)}, u32[]{:S(2)}, u32[]{:S(2)}) collective-permute-start(f32[200,128]{1,0:T(8,128)S(1)} %get-tuple-element.132), channel_id=1, source_target_pairs={{0,14},{1,15},{2,12},{3,13},{4,10},{5,11},{6,8},{7,9},{8,6},{9,7},... | collective-permute-start | bytes 307208 | tf_op jit(solution)/shard_map/ppermute | solution.py:471
  22.5 2.1 %collective-permute-start.24 = (f32[200,128]{1,0:T(8,128)S(1)}, f32[200,128]{1,0:T(8,128)S(1)}, u32[]{:S(2)}, u32[]{:S(2)}) collective-permute-start(f32[200,128]{1,0:T(8,128)S(1)} %get-tuple-element.117), channel_id=1, source_target_pairs={{0,2},{1,3},{2,0},{3,1},{4,6},{5,7},{6,4},{7,5},{8,10},{9,11},{10,... | collective-permute-start | bytes 307208 | tf_op jit(solution)/shard_map/ppermute | solution.py:471
  24.7 1.8 %collective-permute-start.26 = (f32[200,128]{1,0:T(8,128)S(1)}, f32[200,128]{1,0:T(8,128)S(1)}, u32[]{:S(2)}, u32[]{:S(2)}) collective-permute-start(f32[200,128]{1,0:T(8,128)S(1)} %get-tuple-element.119), channel_id=1, source_target_pairs={{0,6},{1,7},{2,4},{3,5},{4,2},{5,3},{6,0},{7,1},{8,14},{9,15},{10,... | collective-permute-start | bytes 307208 | tf_op jit(solution)/shard_map/ppermute | solution.py:471
  28.3 1.2 %collective-permute-done.37.refs_7_ = f32[200,128]{1,0:T(8,128)S(1)} collective-permute-done((f32[200,128]{1,0:T(8,128)S(1)}, f32[200,128]{1,0:T(8,128)S(1)}, u32[]{:S(2)}, u32[]{:S(2)}) %collective-permute-start.37) | collective-permute-done | bytes 102432 | tf_op jit(solution)/shard_map/ppermute | solution.py:471
  30.2 2.7 %collective-permute-start.39 = (f32[264,128]{1,0:T(8,128)S(1)}, f32[264,128]{1,0:T(8,128)S(1)}, u32[]{:S(2)}, u32[]{:S(2)}) collective-permute-start(f32[264,128]{1,0:T(8,128)S(1)} %get-tuple-element.135), channel_id=1, source_target_pairs={{0,16},{1,17},{2,18},{3,19},{4,20},{5,21},{6,22},{7,23},{8,24},{9,... | collective-permute-start | bytes 405512 | tf_op jit(solution)/shard_map/ppermute | solution.py:471
  33.2 1.1 %collective-permute-start.28 = (f32[200,128]{1,0:T(8,128)S(1)}, f32[200,128]{1,0:T(8,128)S(1)}, u32[]{:S(2)}, u32[]{:S(2)}) collective-permute-start(f32[200,128]{1,0:T(8,128)S(1)} %get-tuple-element.121), channel_id=1, source_target_pairs={{0,10},{1,11},{2,8},{3,9},{4,14},{5,15},{6,12},{7,13},{8,2},{9,3},... | collective-permute-start | bytes 307208 | tf_op jit(solution)/shard_map/ppermute | solution.py:471
  35.2 3.5 %collective-permute-start.30 = (f32[200,128]{1,0:T(8,128)S(1)}, f32[200,128]{1,0:T(8,128)S(1)}, u32[]{:S(2)}, u32[]{:S(2)}) collective-permute-start(f32[200,128]{1,0:T(8,128)S(1)} %get-tuple-element.123), channel_id=1, source_target_pairs={{0,14},{1,15},{2,12},{3,13},{4,10},{5,11},{6,8},{7,9},{8,6},{9,7},... | collective-permute-start | bytes 307208 | tf_op jit(solution)/shard_map/ppermute | solution.py:471
  38.7 5.2 %collective-permute-done.28.refs_5_ = f32[200,128]{1,0:T(8,128)S(1)} collective-permute-done((f32[200,128]{1,0:T(8,128)S(1)}, f32[200,128]{1,0:T(8,128)S(1)}, u32[]{:S(2)}, u32[]{:S(2)}) %collective-permute-start.28) | collective-permute-done | bytes 102432 | tf_op jit(solution)/shard_map/ppermute | solution.py:471
  44.8 1.2 %collective-permute-done.30.refs_7_ = f32[200,128]{1,0:T(8,128)S(1)} collective-permute-done((f32[200,128]{1,0:T(8,128)S(1)}, f32[200,128]{1,0:T(8,128)S(1)}, u32[]{:S(2)}, u32[]{:S(2)}) %collective-permute-start.30) | collective-permute-done | bytes 102432 | tf_op jit(solution)/shard_map/ppermute | solution.py:471
  46.8 1.2 %collective-permute-start.43 = (f32[264,128]{1,0:T(8,128)S(1)}, f32[264,128]{1,0:T(8,128)S(1)}, u32[]{:S(2)}, u32[]{:S(2)}) collective-permute-start(f32[264,128]{1,0:T(8,128)S(1)} %add.17.refs_1_), channel_id=1, source_target_pairs={{0,2},{1,3},{2,0},{3,1},{4,6},{5,7},{6,4},{7,5},{8,10},{9,11},{10,... | collective-permute-start | bytes 405512 | tf_op jit(solution)/shard_map/ppermute | solution.py:471
  47.9 1.0 %collective-permute-start.42 = (f32[264,128]{1,0:T(8,128)S(1)}, f32[264,128]{1,0:T(8,128)S(1)}, u32[]{:S(2)}, u32[]{:S(2)}) collective-permute-start(f32[264,128]{1,0:T(8,128)S(1)} %add.16.refs_0_), channel_id=1, source_target_pairs={{0,2},{1,3},{2,0},{3,1},{4,6},{5,7},{6,4},{7,5},{8,10},{9,11},{10,... | collective-permute-start | bytes 405512 | tf_op jit(solution)/shard_map/ppermute | solution.py:471
  48.9 1.2 %owned_rows.1 = s32[8,512]{1,0:T(8,128)S(1)} custom-call(s32[3]{0:T(128)S(1)} %pad_add_fusion.me_ref, s32[8,128]{1,0:T(8,128)S(1)} %dynamic-slice_bitcast_fusion.owner_ref), custom_call_target="tpu_custom_call" | custom-call | tf_op jit(solution)/shard_map/owned_rows/pallas_call | solution.py:330
  50.7 1.6 %collective-permute-done.43.refs_1_.refs_3_ = f32[264,128]{1,0:T(8,128)S(1)} collective-permute-done((f32[264,128]{1,0:T(8,128)S(1)}, f32[264,128]{1,0:T(8,128)S(1)}, u32[]{:S(2)}, u32[]{:S(2)}) %collective-permute-start.43) | collective-permute-done | bytes 135200 | tf_op jit(solution)/shard_map/ppermute | solution.py:471
  52.3 1.4 %collective-permute-done.42.refs_0_.refs_2_ = f32[264,128]{1,0:T(8,128)S(1)} collective-permute-done((f32[264,128]{1,0:T(8,128)S(1)}, f32[264,128]{1,0:T(8,128)S(1)}, u32[]{:S(2)}, u32[]{:S(2)}) %collective-permute-start.42) | collective-permute-done | bytes 135200 | tf_op jit(solution)/shard_map/ppermute | solution.py:471
  53.8 1.5 %early.3 = (f32[512,128]{1,0:T(8,128)S(1)}, f32[512,128]{1,0:T(8,128)S(1)}, s32[1]{0:T(128)}) custom-call(s32[3]{0:T(128)S(1)} %pad_add_fusion.me_ref, s32[1024]{0:T(1024)S(1)} %bitcast.26, f32[264,128]{1,0:T(8,128)S(1)} %add.16.refs_0_, f32[264,128]{1,0:T(8,128)S(1)} %add.17.refs_1_, f32[264,128]{1,0:T(8,128)S(1)} %collective-permute-done.40.refs_2_.refs_4_, ...), custom_call_target="tpu_custom_call" | custom-call | tf_op jit(solution)/shard_map/early/pallas_call | solution.py:382
  56.7 2.0 %late.3 = (f32[512,256]{1,0:T(8,128)}, f32[1024,256]{1,0:T(8,128)}) custom-call(s32[3]{0:T(128)S(1)} %pad_add_fusion.me_ref, s32[1024]{0:T(1024)S(1)} %bitcast.28, f32[512,128]{1,0:T(8,128)S(1)} %middle.3.own_rows, f32[512,128]{1,0:T(8,128)S(1)} %get-tuple-element.138.before_ref, f32[264,128]{1,0:T(8,128)S(1)} %add.16.refs_0_, f32[264,128]{1,0:T(8,128)S(1)} %add.17.refs_1_, ...), custom_call_target="tpu_custom_call" | custom-call | tf_op jit(solution)/shard_map/late/pallas_call | solution.py:433
  (48 shorter events, 8.3 us)
Async XLA Ops:
  0.6 48.3 %copy-start = (s32[8192]{0:T(1024)S(1)}, s32[8192]{0:T(1024)}, u32[]{:S(2)}) copy-start(s32[8192]{0:T(1024)} %param.13) | copy-start | bytes 98308
  7.5 2.7 %collective-permute-start.23 = (f32[1792,128]{1,0:T(8,128)S(1)}, f32[1792,128]{1,0:T(8,128)S(1)}, u32[]{:S(2)}, u32[]{:S(2)}) collective-permute-start(f32[1792,128]{1,0:T(8,128)S(1)} %get-tuple-element.115), channel_id=1, source_target_pairs={{0,1},{1,0},{2,3},{3,2},{4,5},{5,4},{6,7},{7,6},{8,9},{9,8},{10,11... | collective-permute-start | bytes 2752520 | tf_op jit(solution)/shard_map/ppermute | solution.py:471
  10.8 7.9 %collective-permute-start.31 = (f32[200,128]{1,0:T(8,128)S(1)}, f32[200,128]{1,0:T(8,128)S(1)}, u32[]{:S(2)}, u32[]{:S(2)}) collective-permute-start(f32[200,128]{1,0:T(8,128)S(1)} %get-tuple-element.126), channel_id=1, source_target_pairs={{0,2},{1,3},{2,0},{3,1},{4,6},{5,7},{6,4},{7,5},{8,10},{9,11},{10,... | collective-permute-start | bytes 307208 | tf_op jit(solution)/shard_map/ppermute | solution.py:471
  13.7 7.5 %collective-permute-start.32 = (f32[200,128]{1,0:T(8,128)S(1)}, f32[200,128]{1,0:T(8,128)S(1)}, u32[]{:S(2)}, u32[]{:S(2)}) collective-permute-start(f32[200,128]{1,0:T(8,128)S(1)} %get-tuple-element.127), channel_id=1, source_target_pairs={{0,4},{1,5},{2,6},{3,7},{4,0},{5,1},{6,2},{7,3},{8,12},{9,13},{10,... | collective-permute-start | bytes 307208 | tf_op jit(solution)/shard_map/ppermute | solution.py:471
  15.3 7.3 %collective-permute-start.33 = (f32[200,128]{1,0:T(8,128)S(1)}, f32[200,128]{1,0:T(8,128)S(1)}, u32[]{:S(2)}, u32[]{:S(2)}) collective-permute-start(f32[200,128]{1,0:T(8,128)S(1)} %get-tuple-element.128), channel_id=1, source_target_pairs={{0,6},{1,7},{2,4},{3,5},{4,2},{5,3},{6,0},{7,1},{8,14},{9,15},{10,... | collective-permute-start | bytes 307208 | tf_op jit(solution)/shard_map/ppermute | solution.py:471
  15.3 9.3 %collective-permute-start.34 = (f32[200,128]{1,0:T(8,128)S(1)}, f32[200,128]{1,0:T(8,128)S(1)}, u32[]{:S(2)}, u32[]{:S(2)}) collective-permute-start(f32[200,128]{1,0:T(8,128)S(1)} %get-tuple-element.129), channel_id=1, source_target_pairs={{0,8},{1,9},{2,10},{3,11},{4,12},{5,13},{6,14},{7,15},{8,0},{9,1},... | collective-permute-start | bytes 307208 | tf_op jit(solution)/shard_map/ppermute | solution.py:471
  17.3 7.4 %collective-permute-start.35 = (f32[200,128]{1,0:T(8,128)S(1)}, f32[200,128]{1,0:T(8,128)S(1)}, u32[]{:S(2)}, u32[]{:S(2)}) collective-permute-start(f32[200,128]{1,0:T(8,128)S(1)} %get-tuple-element.130), channel_id=1, source_target_pairs={{0,10},{1,11},{2,8},{3,9},{4,14},{5,15},{6,12},{7,13},{8,2},{9,3},... | collective-permute-start | bytes 307208 | tf_op jit(solution)/shard_map/ppermute | solution.py:471
  18.7 8.8 %collective-permute-start.36 = (f32[200,128]{1,0:T(8,128)S(1)}, f32[200,128]{1,0:T(8,128)S(1)}, u32[]{:S(2)}, u32[]{:S(2)}) collective-permute-start(f32[200,128]{1,0:T(8,128)S(1)} %get-tuple-element.131), channel_id=1, source_target_pairs={{0,12},{1,13},{2,14},{3,15},{4,8},{5,9},{6,10},{7,11},{8,4},{9,5},... | collective-permute-start | bytes 307208 | tf_op jit(solution)/shard_map/ppermute | solution.py:471
  21.2 8.3 %collective-permute-start.37 = (f32[200,128]{1,0:T(8,128)S(1)}, f32[200,128]{1,0:T(8,128)S(1)}, u32[]{:S(2)}, u32[]{:S(2)}) collective-permute-start(f32[200,128]{1,0:T(8,128)S(1)} %get-tuple-element.132), channel_id=1, source_target_pairs={{0,14},{1,15},{2,12},{3,13},{4,10},{5,11},{6,8},{7,9},{8,6},{9,7},... | collective-permute-start | bytes 307208 | tf_op jit(solution)/shard_map/ppermute | solution.py:471
  22.5 10.4 %collective-permute-start.24 = (f32[200,128]{1,0:T(8,128)S(1)}, f32[200,128]{1,0:T(8,128)S(1)}, u32[]{:S(2)}, u32[]{:S(2)}) collective-permute-start(f32[200,128]{1,0:T(8,128)S(1)} %get-tuple-element.117), channel_id=1, source_target_pairs={{0,2},{1,3},{2,0},{3,1},{4,6},{5,7},{6,4},{7,5},{8,10},{9,11},{10,... | collective-permute-start | bytes 307208 | tf_op jit(solution)/shard_map/ppermute | solution.py:471
  24.6 8.6 %collective-permute-start.25 = (f32[200,128]{1,0:T(8,128)S(1)}, f32[200,128]{1,0:T(8,128)S(1)}, u32[]{:S(2)}, u32[]{:S(2)}) collective-permute-start(f32[200,128]{1,0:T(8,128)S(1)} %get-tuple-element.118), channel_id=1, source_target_pairs={{0,4},{1,5},{2,6},{3,7},{4,0},{5,1},{6,2},{7,3},{8,12},{9,13},{10,... | collective-permute-start | bytes 307208 | tf_op jit(solution)/shard_map/ppermute | solution.py:471
  24.7 9.6 %collective-permute-start.26 = (f32[200,128]{1,0:T(8,128)S(1)}, f32[200,128]{1,0:T(8,128)S(1)}, u32[]{:S(2)}, u32[]{:S(2)}) collective-permute-start(f32[200,128]{1,0:T(8,128)S(1)} %get-tuple-element.119), channel_id=1, source_target_pairs={{0,6},{1,7},{2,4},{3,5},{4,2},{5,3},{6,0},{7,1},{8,14},{9,15},{10,... | collective-permute-start | bytes 307208 | tf_op jit(solution)/shard_map/ppermute | solution.py:471
  27.5 7.7 %collective-permute-start.27 = (f32[200,128]{1,0:T(8,128)S(1)}, f32[200,128]{1,0:T(8,128)S(1)}, u32[]{:S(2)}, u32[]{:S(2)}) collective-permute-start(f32[200,128]{1,0:T(8,128)S(1)} %get-tuple-element.120), channel_id=1, source_target_pairs={{0,8},{1,9},{2,10},{3,11},{4,12},{5,13},{6,14},{7,15},{8,0},{9,1},... | collective-permute-start | bytes 307208 | tf_op jit(solution)/shard_map/ppermute | solution.py:471
  30.2 16.5 %collective-permute-start.39 = (f32[264,128]{1,0:T(8,128)S(1)}, f32[264,128]{1,0:T(8,128)S(1)}, u32[]{:S(2)}, u32[]{:S(2)}) collective-permute-start(f32[264,128]{1,0:T(8,128)S(1)} %get-tuple-element.135), channel_id=1, source_target_pairs={{0,16},{1,17},{2,18},{3,19},{4,20},{5,21},{6,22},{7,23},{8,24},{9,... | collective-permute-start | bytes 405512 | tf_op jit(solution)/shard_map/ppermute | solution.py:471
  32.9 15.0 %collective-permute-start.38 = (f32[264,128]{1,0:T(8,128)S(1)}, f32[264,128]{1,0:T(8,128)S(1)}, u32[]{:S(2)}, u32[]{:S(2)}) collective-permute-start(f32[264,128]{1,0:T(8,128)S(1)} %get-tuple-element.133), channel_id=1, source_target_pairs={{0,16},{1,17},{2,18},{3,19},{4,20},{5,21},{6,22},{7,23},{8,24},{9,... | collective-permute-start | bytes 405512 | tf_op jit(solution)/shard_map/ppermute | solution.py:471
  33.2 10.6 %collective-permute-start.28 = (f32[200,128]{1,0:T(8,128)S(1)}, f32[200,128]{1,0:T(8,128)S(1)}, u32[]{:S(2)}, u32[]{:S(2)}) collective-permute-start(f32[200,128]{1,0:T(8,128)S(1)} %get-tuple-element.121), channel_id=1, source_target_pairs={{0,10},{1,11},{2,8},{3,9},{4,14},{5,15},{6,12},{7,13},{8,2},{9,3},... | collective-permute-start | bytes 307208 | tf_op jit(solution)/shard_map/ppermute | solution.py:471
  34.3 10.5 %collective-permute-start.29 = (f32[200,128]{1,0:T(8,128)S(1)}, f32[200,128]{1,0:T(8,128)S(1)}, u32[]{:S(2)}, u32[]{:S(2)}) collective-permute-start(f32[200,128]{1,0:T(8,128)S(1)} %get-tuple-element.122), channel_id=1, source_target_pairs={{0,12},{1,13},{2,14},{3,15},{4,8},{5,9},{6,10},{7,11},{8,4},{9,5},... | collective-permute-start | bytes 307208 | tf_op jit(solution)/shard_map/ppermute | solution.py:471
  35.2 10.8 %collective-permute-start.30 = (f32[200,128]{1,0:T(8,128)S(1)}, f32[200,128]{1,0:T(8,128)S(1)}, u32[]{:S(2)}, u32[]{:S(2)}) collective-permute-start(f32[200,128]{1,0:T(8,128)S(1)} %get-tuple-element.123), channel_id=1, source_target_pairs={{0,14},{1,15},{2,12},{3,13},{4,10},{5,11},{6,8},{7,9},{8,6},{9,7},... | collective-permute-start | bytes 307208 | tf_op jit(solution)/shard_map/ppermute | solution.py:471
  46.8 5.5 %collective-permute-start.43 = (f32[264,128]{1,0:T(8,128)S(1)}, f32[264,128]{1,0:T(8,128)S(1)}, u32[]{:S(2)}, u32[]{:S(2)}) collective-permute-start(f32[264,128]{1,0:T(8,128)S(1)} %add.17.refs_1_), channel_id=1, source_target_pairs={{0,2},{1,3},{2,0},{3,1},{4,6},{5,7},{6,4},{7,5},{8,10},{9,11},{10,... | collective-permute-start | bytes 405512 | tf_op jit(solution)/shard_map/ppermute | solution.py:471
  47.9 5.8 %collective-permute-start.42 = (f32[264,128]{1,0:T(8,128)S(1)}, f32[264,128]{1,0:T(8,128)S(1)}, u32[]{:S(2)}, u32[]{:S(2)}) collective-permute-start(f32[264,128]{1,0:T(8,128)S(1)} %add.16.refs_0_), channel_id=1, source_target_pairs={{0,2},{1,3},{2,0},{3,1},{4,6},{5,7},{6,4},{7,5},{8,10},{9,11},{10,... | collective-permute-start | bytes 405512 | tf_op jit(solution)/shard_map/ppermute | solution.py:471
  50.1 3.6 %collective-permute-start.41 = (f32[264,128]{1,0:T(8,128)S(1)}, f32[264,128]{1,0:T(8,128)S(1)}, u32[]{:S(2)}, u32[]{:S(2)}) collective-permute-start(f32[264,128]{1,0:T(8,128)S(1)} %add.17.refs_1_), channel_id=1, source_target_pairs={{0,1},{1,0},{2,3},{3,2},{4,5},{5,4},{6,7},{7,6},{8,9},{9,8},{10,11... | collective-permute-start | bytes 405512 | tf_op jit(solution)/shard_map/ppermute | solution.py:471
  50.2 3.6 %collective-permute-start.40 = (f32[264,128]{1,0:T(8,128)S(1)}, f32[264,128]{1,0:T(8,128)S(1)}, u32[]{:S(2)}, u32[]{:S(2)}) collective-permute-start(f32[264,128]{1,0:T(8,128)S(1)} %add.16.refs_0_), channel_id=1, source_target_pairs={{0,1},{1,0},{2,3},{3,2},{4,5},{5,4},{6,7},{7,6},{8,9},{9,8},{10,11... | collective-permute-start | bytes 405512 | tf_op jit(solution)/shard_map/ppermute | solution.py:471
  52.3 4.4 %collective-permute-start.45 = (f32[264,128]{1,0:T(8,128)S(1)}, f32[264,128]{1,0:T(8,128)S(1)}, u32[]{:S(2)}, u32[]{:S(2)}) collective-permute-start(f32[264,128]{1,0:T(8,128)S(1)} %collective-permute-done.43.refs_1_.refs_3_), channel_id=1, source_target_pairs={{0,1},{1,0},{2,3},{3,2},{4,5},{5,4},{6,7},{7,6},{8,9},{9,8},{10,11... | collective-permute-start | bytes 405512 | tf_op jit(solution)/shard_map/ppermute | solution.py:471
  53.7 3.0 %collective-permute-start.44 = (f32[264,128]{1,0:T(8,128)S(1)}, f32[264,128]{1,0:T(8,128)S(1)}, u32[]{:S(2)}, u32[]{:S(2)}) collective-permute-start(f32[264,128]{1,0:T(8,128)S(1)} %collective-permute-done.42.refs_0_.refs_2_), channel_id=1, source_target_pairs={{0,1},{1,0},{2,3},{3,2},{4,5},{5,4},{6,7},{7,6},{8,9},{9,8},{10,11... | collective-permute-start | bytes 405512 | tf_op jit(solution)/shard_map/ppermute | solution.py:471
  (4 other events, 51.2 us)
